TPU v7x, 32 devices: a whole 2x2x4 slice. The times are simulated.
32 devices in a mesh: row: 8 (over z, y), col: 4 (over x, core).
Axes of the slice: x: 2, y: 2, z: 4, core: 2. Of those that a mesh axis runs over, the one named last changes fastest.
Arguments:
- lower_panel: float32 [1, 4, 512, 4096], P(None, None, 'col', 'row'), may hold values from -4 to 4, as said below
- right_side: float32 [1, 4096, 4096], P(None, 'row', 'col'), may hold values from -6 to 6
Outputs:
- solution: float32 [4, 512, 4096], P(None, None, 'col')
- updated_rhs: float32 [1, 4096, 4096], P(None, 'row', 'col')
Inputs may be any that keep to these rules, and one draw needn't show every extreme that they name: `lower_panel`: L is lower triangular: entries of tiles L[g, s] with g < s and above the diagonal of L[s, s] are zero; the diagonal entries of L lie between 2 and 4.
All inputs are finite; a program needn't handle non-finite values.
Results may differ from a plain program's by a relative error of at most 0.00017.
Values sent between devices are 32-bit elements; how exact they have to be, the bound alone decides.
A program may use at most 128 MiB of HBM per device.

v0:
```python
import jax
import jax.numpy as jnp
from jax import lax
from jax.sharding import PartitionSpec as P


def from_root(x, axis, root):
    mine = lax.axis_index(axis) == root
    return lax.psum(jnp.where(mine, x, jnp.zeros_like(x)), axis)


def per_device(lower_panel, right_side):
    rounds = lower_panel.shape[0]
    sections = lower_panel.shape[1]
    block = lower_panel.shape[3]
    my_row = lax.axis_index("row")
    row_count = lax.axis_size("row")
    tile_number = jnp.arange(rounds, dtype=jnp.int32) * row_count + my_row
    current = right_side
    collected = []
    for section in range(sections):
        is_owner = my_row == section
        column = lax.dynamic_index_in_dim(lower_panel, section, 1, keepdims=False)
        diag_tile = lax.all_gather(column[0], "col", axis=0, tiled=True).T
        safe_tile = jnp.where(is_owner, diag_tile, jnp.eye(block, dtype=jnp.float32))
        local_solve = lax.linalg.triangular_solve(safe_tile, current[0], left_side=True, lower=True)
        solved = from_root(local_solve, "row", section)
        rows_here = solved
        update = jnp.einsum(
            "rcq,cx->rqx",
            lax.all_gather(column, "col", axis=1, tiled=True),
            rows_here,
            precision=lax.Precision.HIGHEST,
        )
        keep_rows = (tile_number > section)[:, None, None]
        current, solved = (current - jnp.where(keep_rows, update, jnp.float32(0.0)), solved)
        collected.append(solved)
    solutions = jnp.stack(collected)
    return (solutions, current)


def solution(mesh):
    placed = (P(None, None, "col", "row"), P(None, "row", "col"))
    return jax.shard_map(
        per_device,
        mesh=mesh,
        in_specs=placed,
        out_specs=(P(None, None, "col"), P(None, "row", "col")),
        check_vma=False,
    )
```

profile of v0, /device:TPU:0, one launch (start us, length us, event | category | flops | bytes accessed | tf_op | source)
XLA Modules:
  0.0 589.0 jit_solution(5360135936811088487)
XLA Ops:
  11.1 18.7 %all-gather.13.cloned.1.call-done = f32[1,1,512,512]{2,3,1,0:T(8,128)} async-done(((f32[1,1,128,512]{2,3,1,0:T(8,128)}), f32[1,1,512,512]{2,3,1,0:T(8,128)}) %all-gather.13.cloned.1.call-update) | async-done | bytes 1048592 | tf_op jit(solution)/shard_map/all_gather | solution.py:24
  31.9 10.0 %while.8 = (s32[]{:T(128)}, f32[512,512]{1,0:T(8,128)S(1)}, s32[4,2]{0,1:T(2,128)S(1)}, f32[4,128,128]{2,1,0:T(8,128)}, s32[]{:T(128)}) while((s32[]{:T(128)}, f32[512,512]{1,0:T(8,128)S(1)}, s32[4,2]{0,1:T(2,128)S(1)}, f32[4,128,128]{2,1,0:T(8,128)}, s32[]{:T(128)}) %tuple.71), condition=%wide.while_cond, body=%wide.while_body.sunk | while | flops 2 | bytes 132205 | solution.py:26
  41.8 40.7 %custom-call.6 = f32[4,128,128]{1,2,0:T(8,128)} custom-call(f32[4,128,128]{2,1,0:T(8,128)} %get-tuple-element.29), custom_call_target="InvertDiagBlocksLowerTriangular" | custom-call | tf_op jit(solution)/shard_map/triangular_solve/custom-call.1 | solution.py:26
  95.2 7.4 %while.9 = (s32[]{:T(128)}, f32[512,512]{1,0:T(8,128)S(1)}, s32[4,2]{0,1:T(2,128)S(1)}, f32[4,128,128]{2,1,0:T(8,128)S(1)}, s32[]{:T(128)}) while((s32[]{:T(128)}, f32[512,512]{1,0:T(8,128)S(1)}, s32[4,2]{0,1:T(2,128)S(1)}, f32[4,128,128]{2,1,0:T(8,128)S(1)}, s32[]{:T(128)}) %tuple.99), condition=%wide.while_cond.clone, body=%wide.while_body.clone.sunk | while | flops 2 | bytes 131189 | solution.py:26
  102.6 40.4 %custom-call.7 = f32[4,128,128]{1,2,0:T(8,128)} custom-call(f32[4,128,128]{2,1,0:T(8,128)S(1)} %get-tuple-element.30), custom_call_target="InvertDiagBlocksLowerTriangular" | custom-call | tf_op jit(solution)/shard_map/triangular_solve/custom-call.1 | solution.py:26
  143.0 49.6 %all-reduce.5.cloned.1.call-done = f32[512,1024]{1,0:T(8,128)} async-done(((f32[512,1024]{1,0:T(8,128)}), f32[512,1024]{1,0:T(8,128)}) %all-reduce.5.cloned.1.call-update) | async-done | bytes 2097168 | tf_op jit(solution)/shard_map/psum | solution.py:9
  192.6 8.9 %bitcast_subtract_fusion.3 = f32[1,512,1024]{1,2,0:T(8,128)S(1)} fusion(f32[1,512,1024]{1,2,0:T(8,128)} %copy.6, f32[512,1024]{1,0:T(8,128)} %all-reduce.5.cloned.1.call-done, f32[1,1,512,512]{2,3,1,0:T(8,128)S(1)} %copy-done.9, pred[]{:T(512)S(6)} %gt.16), kind=kOutput, calls=%fused_computation.20 | convolution fusion | flops 3222274048 | bytes 7340033 | tf_op jit(solution)/shard_map/rcq,cx->rqx/dot_general | solution.py:29
  208.1 3.9 fusion.30
  217.7 12.0 %while.10 = (s32[]{:T(128)}, f32[512,512]{1,0:T(8,128)}, s32[4,2]{0,1:T(2,128)S(1)}, f32[4,128,128]{2,1,0:T(8,128)S(1)}, s32[]{:T(128)}) while((s32[]{:T(128)}, f32[512,512]{1,0:T(8,128)}, s32[4,2]{0,1:T(2,128)S(1)}, f32[4,128,128]{2,1,0:T(8,128)S(1)}, s32[]{:T(128)}) %tuple.100), condition=%wide.while_cond.clone.1, body=%wide.while_body.clone.1.sunk | while | flops 2 | bytes 131189 | solution.py:26
  230.4 40.1 %custom-call.8 = f32[4,128,128]{1,2,0:T(8,128)S(1)} custom-call(f32[4,128,128]{2,1,0:T(8,128)} %copy-done.15), custom_call_target="InvertDiagBlocksLowerTriangular" | custom-call | tf_op jit(solution)/shard_map/triangular_solve/custom-call.1 | solution.py:26
  270.5 46.1 %all-reduce.7.cloned.1.call-done = f32[512,1024]{1,0:T(8,128)} async-done(((f32[512,1024]{1,0:T(8,128)}), f32[512,1024]{1,0:T(8,128)}) %all-reduce.7.cloned.1.call-update) | async-done | bytes 2097168 | tf_op jit(solution)/shard_map/psum | solution.py:9
  316.6 8.3 %bitcast_subtract_fusion.2 = f32[1,512,1024]{1,2,0:T(8,128)S(1)} fusion(f32[1,512,1024]{1,2,0:T(8,128)S(1)} %bitcast_subtract_fusion.3, f32[512,1024]{1,0:T(8,128)} %all-reduce.7.cloned.1.call-done, f32[1,1,512,512]{2,3,1,0:T(8,128)S(1)} %copy-done.6, pred[]{:T(512)S(6)} %gt.17), kind=kOutput, calls=%fused_computation.19 | convolution fusion | flops 3222274048 | bytes 7340033 | tf_op jit(solution)/shard_map/rcq,cx->rqx/dot_general | solution.py:29
  328.2 2.8 convolution_subtract_fusion.1
  331.6 4.1 fusion.27
  340.7 11.2 %while.11 = (s32[]{:T(128)}, f32[512,512]{1,0:T(8,128)}, s32[4,2]{0,1:T(2,128)S(1)}, f32[4,128,128]{2,1,0:T(8,128)S(1)}, s32[]{:T(128)}) while((s32[]{:T(128)}, f32[512,512]{1,0:T(8,128)}, s32[4,2]{0,1:T(2,128)S(1)}, f32[4,128,128]{2,1,0:T(8,128)S(1)}, s32[]{:T(128)}) %tuple.101), condition=%wide.while_cond.clone.2, body=%wide.while_body.clone.2.sunk | while | flops 2 | bytes 131189 | solution.py:26
  352.6 40.1 %custom-call.9 = f32[4,128,128]{1,2,0:T(8,128)S(1)} custom-call(f32[4,128,128]{2,1,0:T(8,128)} %copy-done.14), custom_call_target="InvertDiagBlocksLowerTriangular" | custom-call | tf_op jit(solution)/shard_map/triangular_solve/custom-call.1 | solution.py:26
  392.7 48.1 %all-reduce.9.cloned.1.call-done = f32[512,1024]{1,0:T(8,128)} async-done(((f32[512,1024]{1,0:T(8,128)}), f32[512,1024]{1,0:T(8,128)}) %all-reduce.9.cloned.1.call-update) | async-done | bytes 2097168 | tf_op jit(solution)/shard_map/psum | solution.py:9
  440.8 8.3 %bitcast_subtract_fusion.1 = f32[1,512,1024]{1,2,0:T(8,128)S(1)} fusion(f32[1,512,1024]{1,2,0:T(8,128)S(1)} %copy-done.1, f32[512,1024]{1,0:T(8,128)} %all-reduce.9.cloned.1.call-done, f32[1,1,512,512]{2,3,1,0:T(8,128)S(1)} %copy-done.7, pred[]{:T(512)S(6)} %gt.18), kind=kOutput, calls=%fused_computation.18 | convolution fusion | flops 3222274048 | bytes 7340033 | tf_op jit(solution)/shard_map/rcq,cx->rqx/dot_general | solution.py:29
  452.4 2.8 convolution_subtract_fusion
  455.8 3.9 fusion.24
  461.9 101.7 %all-reduce.11.cloned.1.call-done = f32[512,1024]{1,0:T(8,128)} async-done(((f32[512,1024]{1,0:T(8,128)}), f32[512,1024]{1,0:T(8,128)}) %all-reduce.11.cloned.1.call-update) | async-done | bytes 2097168 | tf_op jit(solution)/shard_map/psum | solution.py:9
  563.6 9.6 %bitcast_subtract_fusion = f32[1,512,1024]{1,2,0:T(8,128)} fusion(f32[1,512,1024]{1,2,0:T(8,128)S(1)} %copy-done.3, f32[512,1024]{1,0:T(8,128)} %all-reduce.11.cloned.1.call-done, f32[1,1,512,512]{2,3,1,0:T(8,128)S(1)} %copy-done.8, pred[]{:T(512)S(6)} %gt.19), kind=kOutput, calls=%fused_computation.17 | convolution fusion | flops 3222274048 | bytes 7340033 | tf_op jit(solution)/shard_map/rcq,cx->rqx/dot_general | solution.py:29
  573.2 3.0 copy.9
  576.3 5.8 pad_maximum_fusion
  (142 shorter events, 86.9 us)
Async XLA Ops:
  7.2 22.6 %all-gather.13.cloned.1.call-start = ((), (), s32[]{:S(2)}) async-start(), calls=%async_computation.4 | async-start | bytes 1310720 | tf_op jit(solution)/shard_map/all_gather | solution.py:24
  10.0 72.5 %copy-start.4 = (f32[1,512,1024]{2,1,0:T(8,128)S(1)}, f32[1,512,1024]{2,1,0:T(8,128)}, u32[]{:S(2)}) copy-start(f32[1,512,1024]{2,1,0:T(8,128)} %param.5) | copy-start | bytes 6291460
  10.1 83.6 %all-gather.15.cloned.1.call-start = ((), (), s32[]{:S(2)}) async-start(), calls=%async_computation.5 | async-start | bytes 1310720 | tf_op jit(solution)/shard_map/all_gather | solution.py:24
  11.0 181.6 %all-reduce.5.cloned.1.call-start = ((), (), s32[]{:S(2)}) async-start(), calls=%async_computation | async-start | bytes 4194304 | tf_op jit(solution)/shard_map/psum | solution.py:9
  82.6 2.1 copy-start.13
  90.0 0.9 copy-start.11
  90.0 125.3 %all-gather.17.cloned.1.call-start = ((), (), s32[]{:S(2)}) async-start(), calls=%async_computation.6 | async-start | bytes 1310720 | tf_op jit(solution)/shard_map/all_gather | solution.py:24
  91.8 224.8 %all-reduce.7.cloned.1.call-start = ((), (), s32[]{:S(2)}) async-start(), calls=%async_computation.1 | async-start | bytes 4194304 | tf_op jit(solution)/shard_map/psum | solution.py:9
  93.7 98.9 %copy-start.9 = (f32[1,1,512,512]{2,3,1,0:T(8,128)S(1)}, f32[1,1,512,512]{2,3,1,0:T(8,128)}, u32[]{:S(2)}) copy-start(f32[1,1,512,512]{2,3,1,0:T(8,128)} %all-gather.13.cloned.1.call-done) | copy-start | bytes 3145732
  102.6 40.4 %copy-start.10 = (f32[512,512]{1,0:T(8,128)}, f32[512,512]{1,0:T(8,128)S(1)}, u32[]{:S(2)}) copy-start(f32[512,512]{1,0:T(8,128)S(1)} %get-tuple-element.280) | copy-start | bytes 3145732
  192.6 8.9 %copy-start.12 = (f32[4,128,128]{1,2,0:T(8,128)S(1)}, f32[4,128,128]{1,2,0:T(8,128)}, u32[]{:S(2)}) copy-start(f32[4,128,128]{1,2,0:T(8,128)} %custom-call.7) | copy-start | bytes 786436
  214.3 102.4 %copy-start.6 = (f32[1,1,512,512]{2,3,1,0:T(8,128)S(1)}, f32[1,1,512,512]{2,3,1,0:T(8,128)}, u32[]{:S(2)}) copy-start(f32[1,1,512,512]{2,3,1,0:T(8,128)} %all-gather.15.cloned.1.call-done) | copy-start | bytes 3145732
  214.3 123.8 %all-gather.19.cloned.1.call-start = ((), (), s32[]{:S(2)}) async-start(), calls=%async_computation.7 | async-start | bytes 1310720 | tf_op jit(solution)/shard_map/all_gather | solution.py:24
  215.2 225.6 %all-reduce.9.cloned.1.call-start = ((), (), s32[]{:S(2)}) async-start(), calls=%async_computation.2 | async-start | bytes 4194304 | tf_op jit(solution)/shard_map/psum | solution.py:9
  229.7 0.7 copy-start.15
  324.9 6.7 %copy-start = (f32[1,512,1024]{1,2,0:T(8,128)}, f32[1,512,1024]{1,2,0:T(8,128)S(1)}, u32[]{:S(2)}) copy-start(f32[1,512,1024]{1,2,0:T(8,128)S(1)} %bitcast_subtract_fusion.2) | copy-start | bytes 6291460
  337.9 102.9 %copy-start.7 = (f32[1,1,512,512]{2,3,1,0:T(8,128)S(1)}, f32[1,1,512,512]{2,3,1,0:T(8,128)}, u32[]{:S(2)}) copy-start(f32[1,1,512,512]{2,3,1,0:T(8,128)} %all-gather.17.cloned.1.call-done) | copy-start | bytes 3145732
  338.0 102.9 %copy-start.1 = (f32[1,512,1024]{1,2,0:T(8,128)S(1)}, f32[1,512,1024]{1,2,0:T(8,128)}, u32[]{:S(2)}) copy-start(f32[1,512,1024]{1,2,0:T(8,128)} %copy-done) | copy-start | bytes 6291460
  338.0 225.7 %all-reduce.11.cloned.1.call-start = ((), (), s32[]{:S(2)}) async-start(), calls=%async_computation.3 | async-start | bytes 4194304 | tf_op jit(solution)/shard_map/psum | solution.py:9
  351.9 0.7 copy-start.14
  449.1 6.6 %copy-start.2 = (f32[1,512,1024]{1,2,0:T(8,128)}, f32[1,512,1024]{1,2,0:T(8,128)S(1)}, u32[]{:S(2)}) copy-start(f32[1,512,1024]{1,2,0:T(8,128)S(1)} %bitcast_subtract_fusion.1) | copy-start | bytes 6291460
  460.3 103.3 %copy-start.8 = (f32[1,1,512,512]{2,3,1,0:T(8,128)S(1)}, f32[1,1,512,512]{2,3,1,0:T(8,128)}, u32[]{:S(2)}) copy-start(f32[1,1,512,512]{2,3,1,0:T(8,128)} %all-gather.19.cloned.1.call-done) | copy-start | bytes 3145732
  461.9 101.8 %copy-start.3 = (f32[1,512,1024]{1,2,0:T(8,128)S(1)}, f32[1,512,1024]{1,2,0:T(8,128)}, u32[]{:S(2)}) copy-start(f32[1,512,1024]{1,2,0:T(8,128)} %copy-done.2) | copy-start | bytes 6291460
  573.2 3.0 copy-start.5
Sparse Core Ops, SparseCore 0:
  10.2 19.5 all-gather.12
  31.3 16.9 all-gather.14
  90.2 102.4 all-reduce.4
  194.0 16.0 all-gather.16
  214.4 102.1 all-reduce.6
  318.0 16.0 all-gather.18
  338.3 102.4 all-reduce.8
  462.0 101.5 all-reduce.10
where the time goes:
time: 598 us; the launch traced here: 589 us
  waiting for transfers between devices  264 us (44%)
  other arithmetic  181 us (30%)
  matrix products  74.5 us (12%)
  local copies, waits for them, and re-layouts  53.6 us (9%)
  between operations  14.8 us (2%)
    psum x4, waiting for transfers between devices, from_root(): return lax.psum(jnp.where(mine, x, jnp.zeros_like(x)), axis)  246 us
    another operation x9, other arithmetic, per_device(): lax.linalg.triangular_solve(safe_tile, current[0], left_side=True, lower=...  169 us
    another operation x53, local copies, waits for them, and re-layouts, per_device(): lax.linalg.triangular_solve(safe_tile, current[0], left_side=True, lower=...  41.1 us
    another operation x28, matrix products, per_device(): lax.linalg.triangular_solve(safe_tile, current[0], left_side=True, lower=...  39.4 us
    dot_general x4, matrix products, per_device(): jnp.einsum('rcq,cx->rqx', lax.all_gather(column, 'col', axis=1, tiled=Tru...  35.1 us
    all_gather x4, waiting for transfers between devices, per_device(): diag_tile = lax.all_gather(column[0], 'col', axis=0, tiled=True).T  18.7 us
  transfers between devices with their start and end apart: 8, of which 5 were waited for; matrix products, arithmetic and copies ran while one was open for 45% of the time, Pallas kernels for 0%

commit v1 on v0

--- a/solution.py
+++ b/solution.py
@@ -6,7 +6,7 @@
 
 def from_root(x, axis, root):
     mine = lax.axis_index(axis) == root
-    return lax.psum(jnp.where(mine, x, jnp.zeros_like(x)), axis)
+    return jnp.sum(lax.all_gather(jnp.where(mine, x, jnp.zeros_like(x)), axis), axis=0)
 
 
 def per_device(lower_panel, right_side):

time: 598 us -> 1130 us (1.89)
  waiting for transfers between devices: 264 us -> 768 us
  other arithmetic: 181 us -> 216 us
    all_gather x0 -> x4, waiting for transfers between devices: none -> 750 us  [from_root(): lax.all_gather(jnp.where(mine, x, jnp.zeros_like(x)), axis)]
    psum x4 -> x0, waiting for transfers between devices: 246 us -> none  [from_root(): return lax.psum(jnp.where(mine, x, jnp.zeros_like(x)), axis)]
    reduce_sum x0 -> x4, other arithmetic: none -> 37.8 us  [from_root(): jnp.sum(lax.all_gather(jnp.where(mine, x, jnp.zeros_like(x)), axis), axis=0)]
  transfers between devices with their start and end apart: 8 -> 8, of which waited for: 5 -> 5; matrix products, arithmetic and copies ran while one was open for 45% -> 25% of each run, Pallas kernels for 0% -> 0%
where the time goes in v1:
time: 1130 us; the launch traced here: 1120 us
  waiting for transfers between devices  768 us (68%)
  other arithmetic  216 us (19%)
  matrix products  74.4 us (7%)
  local copies, waits for them, and re-layouts  47.5 us (4%)
  between operations  15.1 us (1%)
    all_gather x4, waiting for transfers between devices, from_root(): lax.all_gather(jnp.where(mine, x, jnp.zeros_like(x)), axis)  750 us
    another operation x9, other arithmetic, per_device(): lax.linalg.triangular_solve(safe_tile, current[0], left_side=True, lower=...  166 us
    another operation x28, matrix products, per_device(): lax.linalg.triangular_solve(safe_tile, current[0], left_side=True, lower=...  39.2 us
    reduce_sum x4, other arithmetic, from_root(): jnp.sum(lax.all_gather(jnp.where(mine, x, jnp.zeros_like(x)), axis), axis=0)  37.8 us
    another operation x53, local copies, waits for them, and re-layouts, per_device(): lax.linalg.triangular_solve(safe_tile, current[0], left_side=True, lower=...  35.7 us
    dot_general x4, matrix products, per_device(): jnp.einsum('rcq,cx->rqx', lax.all_gather(column, 'col', axis=1, tiled=Tru...  35.2 us
  transfers between devices with their start and end apart: 8, of which 5 were waited for; matrix products, arithmetic and copies ran while one was open for 25% of the time, Pallas kernels for 0%

profile of v1, /device:TPU:0, one launch (start us, length us, event | category | flops | bytes accessed | tf_op | source)
XLA Modules:
  0.0 1122.1 jit_solution(10997522285641688633)
XLA Ops:
  11.0 18.7 %all-gather.21.cloned.1.call-done = f32[1,1,512,512]{2,3,1,0:T(8,128)} async-done(((f32[1,1,128,512]{2,3,1,0:T(8,128)}), f32[1,1,512,512]{2,3,1,0:T(8,128)}) %all-gather.21.cloned.1.call-update) | async-done | bytes 1048592 | tf_op jit(solution)/shard_map/all_gather | solution.py:24
  31.9 10.4 while.8
  42.2 40.7 %custom-call.6 = f32[4,128,128]{1,2,0:T(8,128)} custom-call(f32[4,128,128]{2,1,0:T(8,128)} %get-tuple-element.29), custom_call_target="InvertDiagBlocksLowerTriangular" | custom-call | tf_op jit(solution)/shard_map/triangular_solve/custom-call.1 | solution.py:26
  95.5 8.6 while.9
  104.1 40.1 %custom-call.7 = f32[4,128,128]{1,2,0:T(8,128)} custom-call(f32[4,128,128]{2,1,0:T(8,128)S(1)} %get-tuple-element.30), custom_call_target="InvertDiagBlocksLowerTriangular" | custom-call | tf_op jit(solution)/shard_map/triangular_solve/custom-call.1 | solution.py:26
  144.2 173.7 %all-gather.23.cloned.1.call-done = f32[4096,1024]{1,0:T(8,128)} async-done(((f32[512,1024]{1,0:T(8,128)}), f32[4096,1024]{1,0:T(8,128)}) %all-gather.23.cloned.1.call-update) | async-done | bytes 16777232 | tf_op jit(solution)/shard_map/all_gather | solution.py:9
  317.9 9.4 reduce_sum.36
  327.3 8.9 bitcast_subtract_fusion.3
  351.4 8.1 while.10
  360.2 40.6 %custom-call.8 = f32[4,128,128]{1,2,0:T(8,128)S(1)} custom-call(f32[4,128,128]{2,1,0:T(8,128)} %copy-done.16), custom_call_target="InvertDiagBlocksLowerTriangular" | custom-call | tf_op jit(solution)/shard_map/triangular_solve/custom-call.1 | solution.py:26
  400.7 173.8 %all-gather.27.cloned.1.call-done = f32[4096,1024]{1,0:T(8,128)} async-done(((f32[512,1024]{1,0:T(8,128)}), f32[4096,1024]{1,0:T(8,128)}) %all-gather.27.cloned.1.call-update) | async-done | bytes 16777232 | tf_op jit(solution)/shard_map/all_gather | solution.py:9
  574.6 9.5 reduce_sum.37
  584.0 8.3 bitcast_subtract_fusion.2
  599.2 3.7 fusion.27
  606.6 8.1 while.11
  614.7 39.5 %custom-call.9 = f32[4,128,128]{1,2,0:T(8,128)S(1)} custom-call(f32[4,128,128]{2,1,0:T(8,128)S(1)} %get-tuple-element.32), custom_call_target="InvertDiagBlocksLowerTriangular" | custom-call | tf_op jit(solution)/shard_map/triangular_solve/custom-call.1 | solution.py:26
  654.3 176.4 %all-gather.31.cloned.1.call-done = f32[4096,1024]{1,0:T(8,128)} async-done(((f32[512,1024]{1,0:T(8,128)}), f32[4096,1024]{1,0:T(8,128)}) %all-gather.31.cloned.1.call-update) | async-done | bytes 16777232 | tf_op jit(solution)/shard_map/all_gather | solution.py:9
  830.7 9.4 reduce_sum.38
  840.2 8.3 bitcast_subtract_fusion.1
  855.4 3.7 fusion.24
  861.3 225.6 %all-gather.35.cloned.1.call-done = f32[4096,1024]{1,0:T(8,128)} async-done(((f32[512,1024]{1,0:T(8,128)}), f32[4096,1024]{1,0:T(8,128)}) %all-gather.35.cloned.1.call-update) | async-done | bytes 16777232 | tf_op jit(solution)/shard_map/all_gather | solution.py:9
  1086.9 9.5 reduce_sum.39
  1096.4 9.6 bitcast_subtract_fusion
  1109.1 5.8 pad_maximum_fusion
  (148 shorter events, 91.4 us)
Async XLA Ops:
  7.2 22.6 %all-gather.21.cloned.1.call-start = ((), (), s32[]{:S(2)}) async-start(), calls=%async_computation | async-start | bytes 1310720 | tf_op jit(solution)/shard_map/all_gather | solution.py:24
  10.0 72.9 %copy-start.5 = (f32[1,512,1024]{2,1,0:T(8,128)S(1)}, f32[1,512,1024]{2,1,0:T(8,128)}, u32[]{:S(2)}) copy-start(f32[1,512,1024]{2,1,0:T(8,128)} %param.5) | copy-start | bytes 6291460
  10.1 84.0 %all-gather.25.cloned.1.call-start = ((), (), s32[]{:S(2)}) async-start(), calls=%async_computation.2 | async-start | bytes 1310720 | tf_op jit(solution)/shard_map/all_gather | solution.py:24
  11.0 306.9 %all-gather.23.cloned.1.call-start = ((), (), s32[]{:S(2)}) async-start(), calls=%async_computation.1 | async-start | bytes 18874368 | tf_op jit(solution)/shard_map/all_gather | solution.py:9
  83.0 2.1 copy-start.15
  90.4 0.9 copy-start.13
  90.5 259.5 %all-gather.29.cloned.1.call-start = ((), (), s32[]{:S(2)}) async-start(), calls=%async_computation.4 | async-start | bytes 1310720 | tf_op jit(solution)/shard_map/all_gather | solution.py:24
  92.2 482.4 %all-gather.27.cloned.1.call-start = ((), (), s32[]{:S(2)}) async-start(), calls=%async_computation.3 | async-start | bytes 18874368 | tf_op jit(solution)/shard_map/all_gather | solution.py:9
  104.1 213.8 %copy-start.11 = (f32[512,512]{1,0:T(8,128)}, f32[512,512]{1,0:T(8,128)S(1)}, u32[]{:S(2)}) copy-start(f32[512,512]{1,0:T(8,128)S(1)} %get-tuple-element.280) | copy-start | bytes 3145732
  317.9 9.4 copy-start.9
  327.3 8.9 copy-start.14
  349.0 256.2 %all-gather.33.cloned.1.call-start = ((), (), s32[]{:S(2)}) async-start(), calls=%async_computation.6 | async-start | bytes 1310720 | tf_op jit(solution)/shard_map/all_gather | solution.py:24
  349.9 480.8 %all-gather.31.cloned.1.call-start = ((), (), s32[]{:S(2)}) async-start(), calls=%async_computation.5 | async-start | bytes 18874368 | tf_op jit(solution)/shard_map/all_gather | solution.py:9
  360.2 214.4 %copy-start.12 = (f32[512,512]{1,0:T(8,128)}, f32[512,512]{1,0:T(8,128)S(1)}, u32[]{:S(2)}) copy-start(f32[512,512]{1,0:T(8,128)S(1)} %get-tuple-element.281) | copy-start | bytes 3145732
  574.6 9.5 copy-start.6
  592.4 6.8 copy-start
  605.1 481.8 %all-gather.35.cloned.1.call-start = ((), (), s32[]{:S(2)}) async-start(), calls=%async_computation.7 | async-start | bytes 18874368 | tf_op jit(solution)/shard_map/all_gather | solution.py:9
  614.7 216.0 %copy-start.10 = (f32[512,512]{1,0:T(8,128)}, f32[512,512]{1,0:T(8,128)S(1)}, u32[]{:S(2)}) copy-start(f32[512,512]{1,0:T(8,128)S(1)} %get-tuple-element.279) | copy-start | bytes 3145732
  830.7 9.4 copy-start.1
  830.7 9.4 copy-start.7
  848.5 6.9 copy-start.2
  1086.9 9.5 copy-start.3
  1086.9 9.5 copy-start.8
  1106.1 3.0 copy-start.4
  (1 other events, 0.7 us)
Sparse Core Ops, SparseCore 0:
  10.2 19.5 all-gather.20
  31.3 16.8 all-gather.24
  90.6 227.2 all-gather.22
  319.3 14.9 all-gather.28
  349.1 225.4 all-gather.26
  576.0 14.9 all-gather.32
  605.2 225.4 all-gather.30
  861.4 225.4 all-gather.34
